TPU v7x, 32 devices: a whole 2x2x4 slice. The times are simulated.
32 devices in a mesh: col: 16 (over z, y, x), sec: 2 (over core).
Axes of the slice: x: 2, y: 2, z: 4, core: 2. Of those that a mesh axis runs over, the one named last changes fastest.
Arguments:
- mps: bfloat16 [16, 96, 6, 6, 96], P('col', 'sec'), may hold values from -6 to 6
- ket: bfloat16 [16, 6, 6, 6, 6, 2], P('col'), may hold values from -6 to 6
- left_proj: bfloat16 [16, 96, 96, 6, 6], P('col', 'sec'), may hold values from -0.109375 to 0.109375
- right_proj: bfloat16 [16, 96, 6, 6, 96], P('col', None, None, None, 'sec'), may hold values from -0.109375 to 0.109375
- bond_charge: int32 [16, 96], P('col'), may hold values from 0 to 5
- new_charge: int32 [16, 96], P('col'), may hold values from 0 to 5
- link_charge: int32 [16, 6], P('col'), may hold values from 0 to 2
- vert_charge: int32 [16, 2, 6], P('col'), may hold values from 0 to 2
Outputs:
- new_mps: bfloat16 [16, 96, 6, 6, 96], P('col', 'sec')
- log_norm: float32 [], replicated
All inputs are finite; a program needn't handle non-finite values.
Results may differ from a plain program's by a relative error of at most 0.0064.
Values may be sent and summed in bfloat16 or wider, within the bound.
A program may use at most 192 MiB of HBM per device.

v0:
```python
import functools

import jax
import jax.numpy as jnp
import numpy as np
from jax import lax
from jax.experimental import pallas as pl
from jax.experimental.pallas import tpu as pltpu
from jax.sharding import PartitionSpec as P

LANES = 128
PACK = 8
F32 = jnp.float32
BF16 = jnp.bfloat16


MESH = pl.DeviceIdType.MESH


def chain(
    legs, phys, block, count, cols, secs,
    left_ref, mps_ref, right_ref, ket_ref, bond_ref, fresh_ref, link_ref, link_sm, vert_sm,
    index_ref, pick2r, pick2c, same2, pick3r, pick3c, same3,
    out_ref, log_ref,
    left_s, mps_s, right_s, up_ref, down_ref, w1, w2, w3, image_s,
    charge_here, charge_next, mps_all, right_all, diff,
    stage, slots, near_send, near_recv, send_sem, recv_sem,
):
    total = cols * secs
    half, chi = left_ref.shape[1:]
    pairs = legs // 2
    rows = legs * PACK
    wide = block * LANES
    me_col, me_sec = lax.axis_index("col"), lax.axis_index("sec")
    me = me_col * secs + me_sec
    before = lax.rem(me_col + cols - 1, cols)
    barrier = pltpu.get_barrier_semaphore()
    step = pl.program_id(0)
    mine = pl.ds(pl.multiple_of(me_sec * half, 16), half)

    def other(k):
        at = lax.rem(me + k, total)
        return at, (at // secs, lax.rem(at, secs))

    def close(k):
        at = me_col * secs + lax.rem(me_sec + k, secs)
        return lax.rem(at - me + total, total)

    def charge_copy():
        return pltpu.make_async_remote_copy(
            src_ref=charge_here, dst_ref=charge_next, send_sem=near_send.at[0], recv_sem=near_recv.at[0],
            device_id=(before, me_sec), device_id_type=MESH,
        )

    def mps_copy(k, source):
        return pltpu.make_async_remote_copy(
            src_ref=mps_ref, dst_ref=mps_all.at[source], send_sem=near_send.at[k],
            recv_sem=near_recv.at[1 + source],
            device_id=(me_col, lax.rem(me_sec + k, secs)), device_id_type=MESH,
        )

    def right_copy():
        return pltpu.make_async_remote_copy(
            src_ref=right_ref, dst_ref=right_all.at[me_sec], send_sem=near_send.at[secs],
            recv_sem=near_recv.at[1 + secs + me_sec],
            device_id=(before, me_sec), device_id_type=MESH,
        )

    def right_pass(k, source):
        return pltpu.make_async_remote_copy(
            src_ref=right_all.at[source], dst_ref=right_all.at[source], send_sem=near_send.at[secs + k],
            recv_sem=near_recv.at[1 + secs + source],
            device_id=(me_col, lax.rem(me_sec + k, secs)), device_id_type=MESH,
        )

    def down_rows(row):
        return jnp.broadcast_to(row, (LANES, LANES)).T

    @pl.when(step == 0)
    def _():
        def greet(k, _):
            pl.semaphore_signal(barrier, inc=1, device_id=other(k)[1], device_id_type=MESH)
            return 0

        lax.fori_loop(1, total, greet, 0)
        charge_here[...] = jnp.zeros_like(charge_here)
        charge_here[0:1, 0:chi] = bond_ref[...]
        charge_here[1:2, 0:chi] = fresh_ref[...]
        charge_here[2:3, 0:legs] = link_ref[...]
        here = charge_here[...].astype(F32)
        diff[...] = down_rows(here[1:2]) - here[0:1]
        left_s[...] = jnp.zeros_like(left_s)
        delta = diff[mine, 0:chi]
        for l in range(legs):
            for m in range(legs):
                gap = (link_sm[0, l] - link_sm[0, m]).astype(F32)
                value = jnp.where(delta == gap, left_ref[l * legs + m].astype(F32), 0.0)
                left_s[pl.ds(m * PACK + l, half, stride=rows), :] = value
        mps_s[...] = jnp.zeros_like(mps_s)
        pl.semaphore_wait(barrier, total - 1)
        charge_copy().start()
        for k in range(1, secs):
            mps_copy(k, me_sec).start()
        right_copy().start()
        charge_copy().wait_recv()
        after = charge_next[...].astype(F32)
        diff[...] = after[0:1] - down_rows(here[0:1])

        def place(which, source):
            at = pl.ds(pl.multiple_of(which * half, 16), half)
            delta = diff[at, 0:chi]
            for u in range(legs):
                for v in range(legs):
                    gap = (vert_sm[0, u] - vert_sm[0, v]).astype(F32)
                    uv = u * legs + v
                    value = jnp.where(delta == gap, source[uv].astype(F32), 0.0)
                    mps_s[at, uv * LANES : uv * LANES + chi] = value.astype(BF16)

        place(me_sec, mps_ref)
        lower = index_ref[1].astype(F32)
        upper = jnp.zeros_like(lower)
        for i in range(legs):
            lower += jnp.where(index_ref[0] == i, vert_sm[1, i].astype(F32), 0.0)
            lower += jnp.where(index_ref[2] == i, after[2:3, i : i + 1], 0.0)
            upper += jnp.where(index_ref[3] == i, vert_sm[0, i].astype(F32), 0.0)
            upper += jnp.where(index_ref[4] == i, link_sm[0, i].astype(F32), 0.0)
        ket = jnp.where(upper == lower, ket_ref[...].astype(F32), 0.0).astype(BF16)
        grown = jnp.dot(pick2r[...], ket, preferred_element_type=F32).astype(BF16)
        up_ref[...] = (jnp.dot(grown, pick2c[...], preferred_element_type=F32) * same2[...]).astype(BF16)
        low = jnp.zeros(down_ref.shape, F32)
        for p in range(phys):
            grown = jnp.dot(pick3r[p], ket, preferred_element_type=F32).astype(BF16)
            low += jnp.dot(grown, pick3c[p], preferred_element_type=F32)
        down_ref[...] = (low * same3[...]).astype(BF16)
        for k in range(1, secs):
            source = lax.rem(me_sec + k, secs)
            mps_copy(k, source).wait_recv()
            place(source, mps_all.at[source])

    @pl.when(step == pl.num_programs(0) // 2)
    def _():
        right_copy().wait_recv()
        for k in range(1, secs):
            right_pass(k, me_sec).start()

    base = pl.multiple_of(step * (block * rows), block * rows)
    left = left_s[pl.ds(base, block * rows), :].astype(BF16)
    for u in range(legs):
        for vp in range(pairs):
            at = (u * legs + 2 * vp) * LANES
            part = jnp.dot(left, mps_s[:, at : at + 2 * LANES], preferred_element_type=F32).astype(BF16)
            for x in range(block):
                for mp in range(pairs):
                    lo = x * rows + mp * 2 * PACK
                    for v2 in range(2):
                        w1[vp, mp, v2 * legs + u, :, x * LANES : (x + 1) * LANES] = part[
                            lo : lo + 2 * PACK, v2 * LANES : (v2 + 1) * LANES
                        ]

    slab = w2.shape[2]

    def second(i, _):
        rhs = w1[i // pairs, i % pairs].reshape(2 * legs * 2 * PACK, wide)
        part = jnp.dot(up_ref[...], rhs, preferred_element_type=F32).astype(BF16)
        w2[:, i] = part.reshape(pairs * legs, slab, wide)
        return 0

    lax.fori_loop(0, pairs * pairs, second, 0, unroll=True)

    for dp in range(pairs):
        for r in range(legs):
            rhs = w2[dp * legs + r].reshape(pairs * pairs * slab, wide)
            part = jnp.dot(down_ref[...], rhs, preferred_element_type=F32).astype(BF16)
            for x in range(block):
                for s in range(legs):
                    lane = (r * legs + s) * LANES
                    row = pl.multiple_of(base + (x * rows + dp * 2 * PACK), 2 * PACK)
                    w3[pl.ds(row, 2 * PACK), lane : lane + LANES] = part[
                        s * 2 * PACK : (s + 1) * 2 * PACK, x * LANES : (x + 1) * LANES
                    ]

    @pl.when(step == pl.num_programs(0) - 1)
    def _():
        after = charge_next[...].astype(F32)
        diff[...] = down_rows(after[1:2]) - after[0:1]
        right_s[...] = jnp.zeros_like(right_s)
        for k in range(1, secs):
            right_pass(k, lax.rem(me_sec + k, secs)).wait_recv()
        for k in range(secs):
            delta = diff[k * half : (k + 1) * half, 0:chi]
            for r in range(legs):
                for s in range(legs):
                    gap = after[2:3, r : r + 1] - after[2:3, s : s + 1]
                    rs = r * legs + s
                    value = jnp.where(delta == gap, right_all[k, rs].astype(F32), 0.0)
                    right_s[k * half : (k + 1) * half, rs * LANES : rs * LANES + chi] = value.astype(BF16)

        def last(i, square):
            at = pl.ds(pl.multiple_of(i * (block * rows), block * rows), block * rows)
            image = lax.dot_general(
                w3[at, :], right_s[...], (((1,), (1,)), ((), ())), preferred_element_type=F32
            )
            image_s[at, :] = image
            return square + jnp.sum((image * image).reshape(block * rows // 8, 8, chi), axis=0)

        square = lax.fori_loop(0, half // block, last, jnp.zeros((8, chi), F32), unroll=True)
        part = jnp.sum(jnp.sum(square, axis=0, keepdims=True), axis=1, keepdims=True)
        stage[...] = jnp.broadcast_to(part, stage.shape)
        slots[me] = jnp.broadcast_to(part, stage.shape)

        def copy_to(k):
            at, where = other(k)
            return pltpu.make_async_remote_copy(
                src_ref=stage,
                dst_ref=slots.at[me],
                send_sem=send_sem.at[k],
                recv_sem=recv_sem.at[me],
                device_id=where,
                device_id_type=pl.DeviceIdType.MESH,
            )

        def send(k, _):
            copy_to(k).start()
            return 0

        def receive(k, _):
            at, where = other(k)
            pltpu.make_async_remote_copy(
                src_ref=stage,
                dst_ref=slots.at[at],
                send_sem=send_sem.at[k],
                recv_sem=recv_sem.at[at],
                device_id=where,
                device_id_type=pl.DeviceIdType.MESH,
            ).wait_recv()
            return 0

        def sent(k, _):
            copy_to(k).wait_send()
            return 0

        lax.fori_loop(1, total, send, 0)
        site = jnp.broadcast_to(part, stage.shape)
        for k in range(1, secs):
            receive(close(k), 0)
            site = site + slots[me_col * secs + lax.rem(me_sec + k, secs)]
        scale = lax.rsqrt(site[0:1, 0:1] / count + 1e-06)
        for d in range(legs):
            for e in range(legs):
                values = image_s[pl.ds(d * PACK + e, half, stride=rows), :]
                out_ref[d * legs + e] = (values * scale).astype(BF16)

        def receive_far(k, _):
            at, _where = other(k)

            @pl.when(at // secs != me_col)
            def _():
                receive(k, 0)

            return 0

        lax.fori_loop(1, total, receive_far, 0)
        sums = jnp.sum(slots[...].reshape(cols, secs, 1, LANES), axis=1) / count
        logs = jnp.sum(0.5 * jnp.log(sums + 1e-06), axis=0) / cols
        log_ref[...] = logs[0:1, 0:1]
        lax.fori_loop(1, total, sent, 0)
        charge_copy().wait_send()
        for k in range(1, secs):
            mps_copy(k, me_sec).wait_send()
        right_copy().wait_send()
        for k in range(1, secs):
            right_pass(k, me_sec).wait_send()


def picks(legs, phys):
    pairs = legs // 2
    eye = lambda n, m=None: np.eye(n, m, dtype=np.float32)
    d, p, r, u, l = np.meshgrid(*[np.arange(n) for n in (legs, phys, legs, legs, legs)], indexing="ij")
    shape = (legs * phys * legs, legs * legs)
    index = np.stack([d, p, r, u, l]).reshape((5,) + shape).astype(np.int32)
    two = np.ones(2, np.float32)
    dd = eye(legs).reshape(pairs, 2, legs)
    pick2r = np.einsum("icD,rR,v,m,pP->ircvmpDPR", dd, eye(legs), two, two, eye(phys)).reshape(-1, shape[0])
    pick2c = np.einsum("uU,lL,w,n->ulwUnL", eye(legs), eye(legs, PACK), two, two).reshape(shape[1], -1)
    same2 = np.einsum("i,c,p,vw,mn,u,l->icvmpwunl", np.ones(pairs * legs), two, np.ones(phys), eye(2), eye(2),
                      np.ones(legs), np.ones(PACK)).reshape(pick2r.shape[0], -1)
    pick3r = np.einsum("sR,c,De,qP->qsceDPR", eye(legs), two, eye(legs, PACK), eye(phys)).reshape(phys, -1, shape[0])
    pick3c = np.einsum("iav,jbm,c,qp->qvmijcabp", dd, dd, two, eye(phys)).reshape(phys, shape[1], -1)
    same3 = np.einsum("s,dc,e,i,a,p->sdeicap", np.ones(legs), eye(2), np.ones(PACK), np.ones(pairs * pairs),
                      np.ones(4), np.ones(phys)).reshape(pick3r.shape[1], -1)
    out = [jnp.asarray(index)]
    return out + [jnp.asarray(a, BF16) for a in (pick2r, pick2c, same2, pick3r, pick3c, same3)]


def local(mps, ket, left_proj, right_proj, bond_charge, new_charge, link_charge, vert_charge):
    half, chi, legs = left_proj.shape[1:4]
    phys = ket.shape[5]
    pairs = legs // 2
    rows = legs * PACK
    block = 12
    wide = block * LANES
    square = legs * legs
    cols, secs = lax.axis_size("col"), lax.axis_size("sec")
    arrays = [
        left_proj[0].transpose(2, 3, 0, 1).reshape(square, half, chi),
        mps[0].transpose(1, 2, 0, 3).reshape(square, half, chi),
        right_proj[0].transpose(1, 2, 3, 0).reshape(square, half, chi),
        ket[0].transpose(2, 4, 3, 0, 1).reshape(square * phys, square),
        bond_charge,
        new_charge,
        link_charge,
    ]
    small = [link_charge, vert_charge[0]]
    tables = picks(legs, phys)
    whole = lambda a: pl.BlockSpec(a.shape, lambda i: (0,) * len(a.shape))
    scalar = pl.BlockSpec(memory_space=pltpu.SMEM)
    outs = [jax.ShapeDtypeStruct((square, half, chi), BF16), jax.ShapeDtypeStruct((1, 1), F32)]
    image, logs = pl.pallas_call(
        functools.partial(chain, legs, phys, block, chi * square * chi, cols, secs),
        grid=(half // block,),
        in_specs=[whole(a) for a in arrays] + [scalar] * 2 + [whole(a) for a in tables],
        out_specs=[whole(a) for a in outs],
        out_shape=outs,
        scratch_shapes=[
            pltpu.VMEM((half * rows, chi), F32),
            pltpu.VMEM((chi, square * LANES), BF16),
            pltpu.VMEM((chi, square * LANES), BF16),
            pltpu.VMEM(tables[3].shape, BF16),
            pltpu.VMEM(tables[6].shape, BF16),
            pltpu.VMEM((pairs, pairs, 2 * legs, 2 * PACK, wide), BF16),
            pltpu.VMEM((pairs * legs, pairs * pairs, 8 * phys, wide), BF16),
            pltpu.VMEM((half * rows, square * LANES), BF16),
            pltpu.VMEM((half * rows, chi), F32),
            pltpu.VMEM((8, LANES), jnp.int32),
            pltpu.VMEM((8, LANES), jnp.int32),
            pltpu.VMEM((secs, square, half, chi), BF16),
            pltpu.VMEM((secs, square, half, chi), BF16),
            pltpu.VMEM((LANES, LANES), F32),
            pltpu.VMEM((1, LANES), F32),
            pltpu.VMEM((cols * secs, 1, LANES), F32),
            pltpu.SemaphoreType.DMA((2 * secs,)),
            pltpu.SemaphoreType.DMA((1 + 2 * secs,)),
            pltpu.SemaphoreType.DMA((cols * secs,)),
            pltpu.SemaphoreType.DMA((cols * secs,)),
        ],
        compiler_params=pltpu.CompilerParams(
            dimension_semantics=("arbitrary",),
            vmem_limit_bytes=60 * 1024 * 1024,
            collective_id=0,
            has_side_effects=True,
        ),
    )(*arrays, *small, *tables)
    new_mps = image.reshape(legs, legs, half, chi).transpose(2, 0, 1, 3)[None]
    return (new_mps, logs[0, 0])


def solution(mesh):
    placed = (
        P("col", "sec", None, None, None),
        P("col", None, None, None, None, None),
        P("col", "sec", None, None, None),
        P("col", None, None, None, "sec"),
        P("col", None),
        P("col", None),
        P("col", None),
        P("col", None, None),
    )
    return jax.shard_map(
        local,
        mesh=mesh,
        in_specs=placed,
        out_specs=(P("col", "sec", None, None, None), P()),
        check_vma=False,
    )
```

profile of v0, /device:TPU:0, one launch (start us, length us, event | category | flops | bytes accessed | tf_op | source)
XLA Modules:
  0.0 51.9 jit_solution(3057870471838500576)
XLA Ops:
  0.6 1.0 %reshape.22 = bf16[72,36]{0,1:T(8,128)(2,1)S(1)} reshape(bf16[6,2,6,6,6]{2,1,0,4,3:T(2,128)(2,1)} %bitcast.31) | data formatting | bytes 10368 | tf_op jit(solution)/shard_map/reshape | solution.py:308
  1.7 0.7 %copy.18.ket_ref = bf16[72,36]{1,0:T(8,128)(2,1)} copy(bf16[72,36]{0,1:T(8,128)(2,1)S(1)} %reshape.22) | data formatting | bytes 10368 | tf_op jit(solution)/shard_map/reshape | solution.py:308
  2.4 45.9 %shard_map.158 = (bf16[36,48,96]{2,1,0:T(8,128)(2,1)}, f32[1,1]{1,0:T(1,128)}) custom-call(bf16[36,48,96]{2,1,0:T(8,128)(2,1)} %bitcast.27, bf16[36,48,96]{2,1,0:T(8,128)(2,1)} %bitcast.28, bf16[36,48,96]{2,1,0:T(8,128)(2,1)} %bitcast.29, bf16[72,36]{1,0:T(8,128)(2,1)} %copy.18.ket_ref, s32[1,96]{1,0:T(1,128)} %bond_ref.1, s32[1,96]{1,0:T(1,128)} %fresh_ref.1, ...), custom_call_target="tpu_custom_call" | custom-call | tf_op jit(solution)/shard_map/pallas_call | solution.py:318
  48.3 1.8 %copy.21 = bf16[1,48,6,6,96]{4,1,3,2,0:T(8,128)(2,1)} copy(bf16[1,48,6,6,96]{4,1,3,2,0:T(8,128)(2,1)} %bitcast.30) | data formatting | bytes 663552
where the time goes:
time: 52.1 us; the launch traced here: 51.9 us
  Pallas kernels  45.9 us (88%)
  local copies, waits for them, and re-layouts  3.55 us (7%)
  between operations  2.44 us (5%)
    pallas_call x1, Pallas kernels, local(): pl.pallas_call(functools.partial(chain, legs, phys, block, chi * square *...  45.9 us
    unnamed x1, local copies, waits for them, and re-layouts  1.8 us
    reshape x2, local copies, waits for them, and re-layouts, local(): ket[0].transpose(2, 4, 3, 0, 1).reshape(square * phys, square)  1.75 us

commit v1 on v0

v1 whole, which is shorter than its diff:
```python
import functools
import math

import jax
import jax.numpy as jnp
from jax import lax
from jax.experimental import pallas as pl
from jax.experimental.pallas import tpu as pltpu
from jax.sharding import PartitionSpec as P

LANES = 128
F32 = jnp.float32
BF16 = jnp.bfloat16
MESH = pl.DeviceIdType.MESH


def layout(chi, half, legs):
    span = math.lcm(chi, LANES)
    group, tiles = span // chi, span // LANES
    pieces = []
    for t in range(tiles):
        row = []
        for g in range(group):
            lo, hi = max(LANES * t, chi * g), min(LANES * (t + 1), chi * (g + 1))
            if lo < hi:
                row.append((g, lo - LANES * t, hi - LANES * t))
        pieces.append(row)
    assert all(len(row) == 2 and row[1][0] == row[0][0] + 1 for row in pieces)
    assert half % (2 * group) == 0 and half % 16 == 0 and chi <= LANES and legs % 2 == 0
    pad = -(-legs * legs // 8) * 8
    return group, tiles, half // group, pad, pieces


def chain(
    legs, phys, count, cols, secs,
    left_hbm, mps_hbm, right_hbm, ket_ref, bond_ref, fresh_ref, link_ref, link_sm, vert_sm,
    out_ref, log_ref,
    left_v, mps_all, right_all, left_s, left_b, rhs1, rhs4, raw_s, whole_s, w1, w2, w3, image_s, clean_s,
    charge_here, charge_next, diff, rowkey, lanekey,
    stage, slots, local_sem, near_send, near_recv, send_sem, recv_sem,
):
    total = cols * secs
    square = legs * legs
    half, chi = left_v.shape[1:]
    group, tiles, quads, pad, pieces = layout(chi, half, legs)
    deep = legs * pad
    block = quads * pad
    pairs = legs // 2
    me_col, me_sec = lax.axis_index("col"), lax.axis_index("sec")
    me = me_col * secs + me_sec
    before = lax.rem(me_col + cols - 1, cols)
    barrier = pltpu.get_barrier_semaphore()
    mine = pl.ds(pl.multiple_of(me_sec * half, 16), half)

    def other(k):
        at = lax.rem(me + k, total)
        return at, (at // secs, lax.rem(at, secs))

    def close(k):
        at = me_col * secs + lax.rem(me_sec + k, secs)
        return lax.rem(at - me + total, total)

    def charge_copy():
        return pltpu.make_async_remote_copy(
            src_ref=charge_here, dst_ref=charge_next, send_sem=near_send.at[0], recv_sem=near_recv.at[0],
            device_id=(before, me_sec), device_id_type=MESH,
        )

    def mps_copy(k, source):
        return pltpu.make_async_remote_copy(
            src_ref=mps_hbm, dst_ref=mps_all.at[source], send_sem=near_send.at[k],
            recv_sem=near_recv.at[1 + source],
            device_id=(me_col, lax.rem(me_sec + k, secs)), device_id_type=MESH,
        )

    def right_copy():
        return pltpu.make_async_remote_copy(
            src_ref=right_hbm, dst_ref=right_all.at[me_sec], send_sem=near_send.at[secs],
            recv_sem=near_recv.at[1 + secs + me_sec],
            device_id=(before, me_sec), device_id_type=MESH,
        )

    def right_pass(k, source):
        return pltpu.make_async_remote_copy(
            src_ref=right_all.at[source], dst_ref=right_all.at[source], send_sem=near_send.at[secs + k],
            recv_sem=near_recv.at[1 + secs + source],
            device_id=(me_col, lax.rem(me_sec + k, secs)), device_id_type=MESH,
        )

    def down_rows(row):
        return jnp.broadcast_to(row, (LANES, LANES)).T

    def over(value, by):
        return jnp.floor((value + 0.5) * (1.0 / by))

    def axis(shape, dim):
        return lax.broadcasted_iota(jnp.int32, shape, dim).astype(F32)

    def chosen(index, values):
        return sum(jnp.where(index == float(i), v, 0.0) for i, v in enumerate(values))

    load_left = pltpu.make_async_copy(left_hbm, left_v, local_sem.at[0])
    load_mps = pltpu.make_async_copy(mps_hbm, mps_all.at[me_sec], local_sem.at[1])
    load_left.start()
    load_mps.start()

    def greet(k, _):
        pl.semaphore_signal(barrier, inc=1, device_id=other(k)[1], device_id_type=MESH)
        return 0

    lax.fori_loop(1, total, greet, 0)
    charge_here[...] = jnp.zeros_like(charge_here)
    charge_here[0:1, 0:chi] = bond_ref[...]
    charge_here[1:2, 0:chi] = fresh_ref[...]
    charge_here[2:3, 0:legs] = link_ref[...]
    here = charge_here[...].astype(F32)
    diff[...] = down_rows(here[1:2]) - here[0:1]
    gaps_here = diff[mine, 0:chi]
    fresh_rows = down_rows(here[1:2])
    left_s[...] = jnp.zeros_like(left_s)
    for t in range(tiles):
        for k in range(2):
            rhs1[t, k * LANES + chi : (k + 1) * LANES] = jnp.zeros((LANES - chi, square * LANES), BF16)
            rhs4[t, k * LANES + chi : (k + 1) * LANES] = jnp.zeros((LANES - chi, square * LANES), BF16)

    small = (pad, 2 * LANES)
    row_in = axis(small, 0)
    row_mid = over(row_in, legs)
    row_last = row_in - legs * row_mid
    col = axis(small, 1)
    col_top = over(col, pad)
    col_in = col - pad * col_top
    col_mid = over(col_in, legs)
    col_last = col_in - legs * col_mid
    keys = square * legs * phys
    line = axis((pad, keys), 1)
    line_p = over(line, phys)
    line_d = line_p - legs * over(line_p, legs)
    line_p = line - phys * line_p
    tall = (keys, 2 * LANES)
    tall_in = over(axis(tall, 0), legs * phys)
    tall_u = over(tall_in, legs)
    tall_l = tall_in - legs * tall_u
    tall_col = axis(tall, 1)
    tall_top = over(tall_col, pad)
    tall_mid = over(tall_col - pad * tall_top, legs)
    spread_c = jnp.where(jnp.logical_and(tall_u == tall_top, tall_l == tall_mid), 1.0, 0.0).astype(BF16)
    ket = ket_ref[...]
    for r in range(legs):
        lead = jnp.where(axis((pad, legs), 1) == float(r), 1.0, 0.0).astype(BF16)
        grown = lax.dot_general(lead, ket, (((1,), (1,)), ((), ())), preferred_element_type=F32)
        for p in range(phys):
            keep = jnp.logical_and(line_d == row_last[:, 0:1], line_p == float(p))
            picked = jnp.where(keep, grown, 0.0).astype(BF16)
            raw_s[p, r * pad : (r + 1) * pad, :] = jnp.dot(picked, spread_c, preferred_element_type=F32)

    load_left.wait()
    for l in range(legs):
        for m in range(legs):
            gap = (link_sm[0, l] - link_sm[0, m]).astype(F32)
            value = jnp.where(gaps_here == gap, left_v[l * legs + m].astype(F32), 0.0)
            left_s[pl.ds(l * legs + m, half, stride=pad), 0:chi] = value
    left_b[...] = left_s[...].astype(BF16)

    pl.semaphore_wait(barrier, total - 1)
    charge_copy().start()
    for k in range(1, secs):
        mps_copy(k, me_sec).start()
    right_copy().start()

    lane = lax.broadcasted_iota(jnp.int32, (1, LANES), 1)

    def inside(lo, hi):
        return jnp.logical_and(lane >= lo, lane < hi)

    def turned(value):
        rest = jnp.zeros(value.shape[:-1] + (LANES - chi,), value.dtype)
        wide = jnp.concatenate([value, rest], axis=1)
        return [wide if (chi * g) % LANES == 0 else pltpu.roll(wide, (chi * g) % LANES, 1) for g in range(group)]

    def spread(value, dest, at, column):
        rolled = turned(value)
        for t in range(tiles):
            for k, (g, lo, hi) in enumerate(pieces[t]):
                piece = jnp.where(inside(lo, hi), rolled[g], 0.0)
                dest[t, k * LANES + at : k * LANES + at + half, column * LANES : (column + 1) * LANES] = piece.astype(BF16)

    load_mps.wait()
    for k in range(1, secs):
        mps_copy(k, lax.rem(me_sec + k, secs)).wait_recv()
    for k in range(secs):
        for u in range(legs):
            for v in range(legs):
                spread(mps_all[k, u * legs + v].astype(F32), rhs1, k * half, v * legs + u)

    for t in range(tiles):
        lhs = jnp.concatenate([left_b[g * block : (g + 1) * block] for g, _, _ in pieces[t]], axis=1)

        def first(i, _, t=t, lhs=lhs):
            part = jnp.dot(lhs, rhs1[t, :, pl.ds(pl.multiple_of(i * 2 * LANES, 2 * LANES), 2 * LANES)], preferred_element_type=F32)
            for q in range(quads):
                rows = part[q * pad : (q + 1) * pad]
                both = jnp.concatenate([rows[:, :LANES], rows[:, LANES:]], axis=0).astype(BF16)
                at = pl.ds(pl.multiple_of((i % pairs) * 2 * pad, 16), 2 * pad)
                w1[t, q // 2, i // pairs, at, (q % 2) * LANES : (q % 2 + 1) * LANES] = both
            return 0

        lax.fori_loop(0, pairs * legs, first, 0, unroll=True)

    charge_copy().wait_recv()
    after = charge_next[...].astype(F32)

    col_key = chosen(col_top, [vert_sm[0, i].astype(F32) for i in range(legs)])
    col_key += chosen(col_mid, [link_sm[0, i].astype(F32) for i in range(legs)])
    row_key = chosen(row_last, [vert_sm[1, i].astype(F32) for i in range(legs)])
    same = jnp.logical_and(row_mid == col_last, jnp.logical_and(row_in < square, col_in < square))
    for r in range(legs):
        lack = col_key - row_key - after[2:3, r : r + 1]
        value = jnp.zeros(small, F32)
        for p in range(phys):
            value += jnp.where(lack == float(p), raw_s[p, r * pad : (r + 1) * pad, :], 0.0)
        whole_s[r * pad : (r + 1) * pad, :] = jnp.where(same, value, 0.0)
    both_rows = whole_s[:, 0:deep].astype(BF16)

    ups = [vert_sm[0, i].astype(F32) for i in range(legs)]
    mid_key = chosen(row_last, [link_sm[0, i].astype(F32) for i in range(legs)])
    mid_key -= chosen(row_mid, [link_sm[0, i].astype(F32) for i in range(legs)])
    for v in range(legs):
        for u in range(pairs):
            pair = jnp.concatenate([mid_key[:, :LANES] + (ups[2 * u + k] - ups[v]) for k in range(2)], axis=0)
            rowkey[v, u * 2 * pad : (u + 1) * 2 * pad] = pair.astype(BF16)
    turned_next = turned(after[0:1, 0:chi])
    diff[...] = fresh_rows
    for t in range(tiles):
        for q in range(quads):
            key = jnp.zeros((16, LANES), F32)
            for g, lo, hi in pieces[t]:
                own = diff[pl.ds(me_sec * half + g * quads + q, 1), :]
                key += jnp.where(inside(lo, hi), turned_next[g] - own, 0.0)
            lanekey[t, q // 2, :, (q % 2) * LANES : (q % 2 + 1) * LANES] = key.astype(BF16)

    def second(n, slot):
        t, j = n // (quads // 2), n % (quads // 2)
        key = lanekey[t, j][None]
        for vp in range(pairs):
            parts = []
            for k in range(2):
                rows = rowkey[2 * vp + k]
                rows = jnp.concatenate([rows, rows], axis=1).reshape(deep // 16, 16, 2 * LANES)
                value = w1[t, j, 2 * vp + k].reshape(deep // 16, 16, 2 * LANES)
                value = jnp.where(rows == key, value, jnp.zeros_like(value)).reshape(deep, 2 * LANES)
                parts.append(jnp.dot(both_rows, value, preferred_element_type=F32))
            for r in range(legs):
                both = jnp.concatenate([part[r * pad : (r + 1) * pad] for part in parts], axis=0)
                w2[slot, r, vp * 2 * pad : (vp + 1) * 2 * pad, :] = both.astype(BF16)

    def third(n, slot):
        t, j = n // (quads // 2), n % (quads // 2)
        at = pl.ds(pl.multiple_of(j * 2 * pad, 16), 2 * pad)
        for r in range(legs):
            part = jnp.dot(both_rows, w2[slot, r], preferred_element_type=F32)
            for s in range(legs):
                rows = part[s * pad : (s + 1) * pad]
                both = jnp.concatenate([rows[:, :LANES], rows[:, LANES:]], axis=0).astype(BF16)
                w3[t, at, (r * legs + s) * LANES : (r * legs + s + 1) * LANES] = both

    steps = tiles * (quads // 2)

    def middle(n, _):
        second(n, n % 2)
        third(n - 1, (n + 1) % 2)
        return 0

    second(0, 0)
    lax.fori_loop(1, steps // 2, middle, 0, unroll=True)
    right_copy().wait_recv()
    for k in range(1, secs):
        right_pass(k, me_sec).start()
    lax.fori_loop(steps // 2, steps, middle, 0, unroll=True)
    third(steps - 1, (steps - 1) % 2)

    diff[...] = down_rows(after[1:2]) - after[0:1]
    for k in range(1, secs):
        right_pass(k, lax.rem(me_sec + k, secs)).wait_recv()
    for k in range(secs):
        delta = diff[k * half : (k + 1) * half, 0:chi]
        for r in range(legs):
            for s in range(legs):
                gap = after[2:3, r : r + 1] - after[2:3, s : s + 1]
                value = jnp.where(delta == gap, right_all[k, r * legs + s].astype(F32), 0.0)
                spread(value, rhs4, k * half, r * legs + s)

    seen = set()
    for t in range(tiles):
        part = lax.dot_general(w3[t], rhs4[t], (((1,), (1,)), ((), ())), preferred_element_type=F32)
        for k, (g, _, _) in enumerate(pieces[t]):
            value = part[:, k * LANES : (k + 1) * LANES]
            if g in seen:
                value += image_s[g * block : (g + 1) * block]
            seen.add(g)
            image_s[g * block : (g + 1) * block] = value

    diff[...] = fresh_rows + after[1:2]
    odd = diff[mine, 0:chi]
    odd = odd - 2.0 * jnp.floor(odd * 0.5)
    total_sq = jnp.zeros((half, chi), F32)
    for d in range(legs):
        for e in range(legs):
            value = image_s[pl.ds(d * legs + e, half, stride=pad), 0:chi]
            parity = ((vert_sm[1, d] + vert_sm[1, e]) & 1).astype(F32)
            value = jnp.where(odd == parity, value, 0.0)
            clean_s[d * legs + e] = value
            total_sq += value * value
    part = jnp.sum(jnp.sum(total_sq, axis=0, keepdims=True), axis=1, keepdims=True)
    stage[...] = jnp.broadcast_to(part, stage.shape)
    slots[me] = jnp.broadcast_to(part, stage.shape)

    def copy_to(k):
        at, where = other(k)
        return pltpu.make_async_remote_copy(
            src_ref=stage, dst_ref=slots.at[me], send_sem=send_sem.at[k], recv_sem=recv_sem.at[me],
            device_id=where, device_id_type=MESH,
        )

    def send(k, _):
        copy_to(k).start()
        return 0

    def receive(k, _):
        at, where = other(k)
        pltpu.make_async_remote_copy(
            src_ref=stage, dst_ref=slots.at[at], send_sem=send_sem.at[k], recv_sem=recv_sem.at[at],
            device_id=where, device_id_type=MESH,
        ).wait_recv()
        return 0

    def sent(k, _):
        copy_to(k).wait_send()
        return 0

    lax.fori_loop(1, total, send, 0)
    site = jnp.broadcast_to(part, stage.shape)
    for k in range(1, secs):
        receive(close(k), 0)
        site = site + slots[me_col * secs + lax.rem(me_sec + k, secs)]
    scale = lax.rsqrt(site[0:1, 0:1] / count + 1e-06)
    for i in range(square):
        out_ref[i] = (clean_s[i] * scale).astype(BF16)

    def receive_far(k, _):
        at, _where = other(k)

        @pl.when(at // secs != me_col)
        def _():
            receive(k, 0)

        return 0

    lax.fori_loop(1, total, receive_far, 0)
    sums = jnp.sum(slots[...].reshape(cols, secs, 1, LANES), axis=1) / count
    logs = jnp.sum(0.5 * jnp.log(sums + 1e-06), axis=0) / cols
    log_ref[...] = logs[0:1, 0:1]
    lax.fori_loop(1, total, sent, 0)
    charge_copy().wait_send()
    for k in range(1, secs):
        mps_copy(k, me_sec).wait_send()
    right_copy().wait_send()
    for k in range(1, secs):
        right_pass(k, me_sec).wait_send()


def local(mps, ket, left_proj, right_proj, bond_charge, new_charge, link_charge, vert_charge):
    half, chi, legs = left_proj.shape[1:4]
    phys = ket.shape[5]
    assert phys == 2
    square = legs * legs
    cols, secs = lax.axis_size("col"), lax.axis_size("sec")
    group, tiles, quads, pad, pieces = layout(chi, half, legs)
    deep, block = legs * pad, quads * pad
    assert deep <= 2 * LANES
    arrays = [
        left_proj[0].transpose(2, 3, 0, 1).reshape(square, half, chi),
        mps[0].transpose(1, 2, 0, 3).reshape(square, half, chi),
        right_proj[0].transpose(1, 2, 3, 0).reshape(square, half, chi),
        ket[0].transpose(0, 1, 2, 4, 3).reshape(square * legs * phys, legs),
        bond_charge,
        new_charge,
        link_charge,
        link_charge,
        vert_charge[0],
    ]
    far = pl.BlockSpec(memory_space=pl.ANY)
    near = pl.BlockSpec(memory_space=pltpu.VMEM)
    scalar = pl.BlockSpec(memory_space=pltpu.SMEM)
    image, logs = pl.pallas_call(
        functools.partial(chain, legs, phys, chi * square * chi, cols, secs),
        in_specs=[far] * 3 + [near] * 4 + [scalar] * 2,
        out_specs=[near, near],
        out_shape=[jax.ShapeDtypeStruct((square, half, chi), BF16), jax.ShapeDtypeStruct((1, 1), F32)],
        scratch_shapes=[
            pltpu.VMEM((square, half, chi), BF16),
            pltpu.VMEM((secs, square, half, chi), BF16),
            pltpu.VMEM((secs, square, half, chi), BF16),
            pltpu.VMEM((half * pad, LANES), F32),
            pltpu.VMEM((half * pad, LANES), BF16),
            pltpu.VMEM((tiles, 2 * LANES, square * LANES), BF16),
            pltpu.VMEM((tiles, 2 * LANES, square * LANES), BF16),
            pltpu.VMEM((phys, deep, 2 * LANES), F32),
            pltpu.VMEM((deep, 2 * LANES), F32),
            pltpu.VMEM((tiles, quads // 2, legs, deep, 2 * LANES), BF16),
            pltpu.VMEM((2, legs, deep, 2 * LANES), BF16),
            pltpu.VMEM((tiles, block, square * LANES), BF16),
            pltpu.VMEM((half * pad, LANES), F32),
            pltpu.VMEM((square, half, chi), F32),
            pltpu.VMEM((8, LANES), jnp.int32),
            pltpu.VMEM((8, LANES), jnp.int32),
            pltpu.VMEM((LANES, LANES), F32),
            pltpu.VMEM((legs, deep, LANES), BF16),
            pltpu.VMEM((tiles, quads // 2, 16, 2 * LANES), BF16),
            pltpu.VMEM((1, LANES), F32),
            pltpu.VMEM((cols * secs, 1, LANES), F32),
            pltpu.SemaphoreType.DMA((2,)),
            pltpu.SemaphoreType.DMA((2 * secs,)),
            pltpu.SemaphoreType.DMA((1 + 2 * secs,)),
            pltpu.SemaphoreType.DMA((cols * secs,)),
            pltpu.SemaphoreType.DMA((cols * secs,)),
        ],
        compiler_params=pltpu.CompilerParams(
            vmem_limit_bytes=62 * 1024 * 1024,
            collective_id=0,
            has_side_effects=True,
        ),
    )(*arrays)
    new_mps = image.reshape(legs, legs, half, chi).transpose(2, 0, 1, 3)[None]
    return (new_mps, logs[0, 0])


def solution(mesh):
    placed = (
        P("col", "sec", None, None, None),
        P("col", None, None, None, None, None),
        P("col", "sec", None, None, None),
        P("col", None, None, None, "sec"),
        P("col", None),
        P("col", None),
        P("col", None),
        P("col", None, None),
    )
    return jax.shard_map(
        local,
        mesh=mesh,
        in_specs=placed,
        out_specs=(P("col", "sec", None, None, None), P()),
        check_vma=False,
    )
```

time: 52.1 us -> 41.7 us (0.80)
  Pallas kernels: 45.9 us -> 37.3 us
  local copies, waits for them, and re-layouts: 3.55 us -> 1.8 us
    pallas_call x1, Pallas kernels: 45.9 us -> 37.3 us  [local(): pl.pallas_call(functools.partial(chain, legs, phys, chi * square * chi, c...]
    reshape x2 -> x0, local copies, waits for them, and re-layouts: 1.75 us -> none  [local(): ket[0].transpose(2, 4, 3, 0, 1).reshape(square * phys, square)]
where the time goes in v1:
time: 41.7 us; the launch traced here: 41.5 us
  Pallas kernels  37.3 us (89%)
  between operations  2.44 us (6%)
  local copies, waits for them, and re-layouts  1.8 us (4%)
    pallas_call x1, Pallas kernels, local(): pl.pallas_call(functools.partial(chain, legs, phys, chi * square * chi, c...  37.3 us
    unnamed x1, local copies, waits for them, and re-layouts  1.8 us

profile of v1, /device:TPU:0, one launch (start us, length us, event | category | flops | bytes accessed | tf_op | source)
XLA Modules:
  0.0 41.5 jit_solution(16226853709539570244)
XLA Ops:
  0.6 37.3 %shard_map.95 = (bf16[36,48,96]{2,1,0:T(8,128)(2,1)}, f32[1,1]{1,0:T(1,128)}) custom-call(bf16[36,48,96]{2,1,0:T(8,128)(2,1)} %bitcast.27, bf16[36,48,96]{2,1,0:T(8,128)(2,1)} %bitcast.28, bf16[36,48,96]{2,1,0:T(8,128)(2,1)} %bitcast.29, bf16[432,6]{1,0:T(8,128)(2,1)} %bitcast.31, s32[1,96]{1,0:T(1,128)} %bond_ref.1, s32[1,96]{1,0:T(1,128)} %fresh_ref.1, ...), custom_call_target="tpu_custom_call" | custom-call | tf_op jit(solution)/shard_map/pallas_call | solution.py:395
  37.9 1.8 %copy.12 = bf16[1,48,6,6,96]{4,1,3,2,0:T(8,128)(2,1)} copy(bf16[1,48,6,6,96]{4,1,3,2,0:T(8,128)(2,1)} %bitcast.30) | data formatting | bytes 663552

commit v2 on v1

--- a/solution.py
+++ b/solution.py
@@ -37,9 +37,9 @@
     out_ref, log_ref,
     left_v, mps_all, right_all, left_s, left_b, rhs1, rhs4, raw_s, whole_s, w1, w2, w3, image_s, clean_s,
     charge_here, charge_next, diff, rowkey, lanekey,
-    stage, slots, local_sem, near_send, near_recv, send_sem, recv_sem,
+    stage, slots, close_slots, local_sem, near_send, near_recv, chunk_send, chunk_recv, pass_send, pass_recv,
+    known, far_send, far_recv, close_send, close_recv,
 ):
-    total = cols * secs
     square = legs * legs
     half, chi = left_v.shape[1:]
     group, tiles, quads, pad, pieces = layout(chi, half, legs)
@@ -47,18 +47,18 @@
     block = quads * pad
     pairs = legs // 2
     me_col, me_sec = lax.axis_index("col"), lax.axis_index("sec")
-    me = me_col * secs + me_sec
     before = lax.rem(me_col + cols - 1, cols)
     barrier = pltpu.get_barrier_semaphore()
     mine = pl.ds(pl.multiple_of(me_sec * half, 16), half)
 
-    def other(k):
-        at = lax.rem(me + k, total)
-        return at, (at // secs, lax.rem(at, secs))
-
-    def close(k):
-        at = me_col * secs + lax.rem(me_sec + k, secs)
-        return lax.rem(at - me + total, total)
+    chunks = right_all.shape[1]
+    own = right_all.shape[2]
+
+    def column(k):
+        return lax.rem(me_col + k + cols, cols)
+
+    def partner(k):
+        return (me_col, lax.rem(me_sec + k, secs))
 
     def charge_copy():
         return pltpu.make_async_remote_copy(
@@ -70,22 +70,44 @@
         return pltpu.make_async_remote_copy(
             src_ref=mps_hbm, dst_ref=mps_all.at[source], send_sem=near_send.at[k],
             recv_sem=near_recv.at[1 + source],
-            device_id=(me_col, lax.rem(me_sec + k, secs)), device_id_type=MESH,
-        )
-
-    def right_copy():
-        return pltpu.make_async_remote_copy(
-            src_ref=right_hbm, dst_ref=right_all.at[me_sec], send_sem=near_send.at[secs],
-            recv_sem=near_recv.at[1 + secs + me_sec],
+            device_id=partner(k), device_id_type=MESH,
+        )
+
+    def right_copy(c):
+        return pltpu.make_async_remote_copy(
+            src_ref=right_hbm.at[pl.ds(c * own, own)], dst_ref=right_all.at[me_sec, c],
+            send_sem=chunk_send.at[c], recv_sem=chunk_recv.at[c],
             device_id=(before, me_sec), device_id_type=MESH,
         )
 
-    def right_pass(k, source):
-        return pltpu.make_async_remote_copy(
-            src_ref=right_all.at[source], dst_ref=right_all.at[source], send_sem=near_send.at[secs + k],
-            recv_sem=near_recv.at[1 + secs + source],
-            device_id=(me_col, lax.rem(me_sec + k, secs)), device_id_type=MESH,
-        )
+    def right_pass(c, k, source):
+        return pltpu.make_async_remote_copy(
+            src_ref=right_all.at[source, c], dst_ref=right_all.at[source, c],
+            send_sem=pass_send.at[c, k], recv_sem=pass_recv.at[c, source],
+            device_id=partner(k), device_id_type=MESH,
+        )
+
+    def arrived(c):
+        right_copy(c).wait_recv()
+        for k in range(1, secs):
+            right_pass(c, k, me_sec).start()
+
+    def passed(c):
+        for k in range(1, secs):
+            right_pass(c, k, lax.rem(me_sec + k, secs)).wait_recv()
+
+    rounds = max(1, (cols // 2 - 1).bit_length())
+
+    def tell(n):
+        if n < rounds:
+            for side in (-1, 1):
+                pl.semaphore_signal(
+                    known.at[n], inc=1, device_id=(column(side * 2**n), me_sec), device_id_type=MESH
+                )
+
+    def hear(n):
+        if n < rounds:
+            pl.semaphore_wait(known.at[n], 2)
 
     def down_rows(row):
         return jnp.broadcast_to(row, (LANES, LANES)).T
@@ -104,11 +126,10 @@
     load_left.start()
     load_mps.start()
 
-    def greet(k, _):
-        pl.semaphore_signal(barrier, inc=1, device_id=other(k)[1], device_id_type=MESH)
-        return 0
-
-    lax.fori_loop(1, total, greet, 0)
+    for k in range(1, secs):
+        pl.semaphore_signal(barrier, inc=1, device_id=partner(k), device_id_type=MESH)
+    for side in (-1, 1):
+        pl.semaphore_signal(barrier, inc=1, device_id=(column(side), me_sec), device_id_type=MESH)
     charge_here[...] = jnp.zeros_like(charge_here)
     charge_here[0:1, 0:chi] = bond_ref[...]
     charge_here[1:2, 0:chi] = fresh_ref[...]
@@ -121,7 +142,50 @@
     for t in range(tiles):
         for k in range(2):
             rhs1[t, k * LANES + chi : (k + 1) * LANES] = jnp.zeros((LANES - chi, square * LANES), BF16)
-            rhs4[t, k * LANES + chi : (k + 1) * LANES] = jnp.zeros((LANES - chi, square * LANES), BF16)
+            for c in range(chunks):
+                rhs4[c][t, k * LANES + chi : (k + 1) * LANES] = jnp.zeros((LANES - chi, own * LANES), BF16)
+
+    lane = lax.broadcasted_iota(jnp.int32, (1, LANES), 1)
+
+    def inside(lo, hi):
+        return jnp.logical_and(lane >= lo, lane < hi)
+
+    def turned(value):
+        rest = jnp.zeros(value.shape[:-1] + (LANES - chi,), value.dtype)
+        wide = jnp.concatenate([value, rest], axis=1)
+        return [wide if (chi * g) % LANES == 0 else pltpu.roll(wide, (chi * g) % LANES, 1) for g in range(group)]
+
+    def spread(value, dest, at, place):
+        rolled = turned(value)
+        for t in range(tiles):
+            for k, (g, lo, hi) in enumerate(pieces[t]):
+                piece = jnp.where(inside(lo, hi), rolled[g], 0.0)
+                dest[t, pl.ds(k * LANES + at, half), place * LANES : (place + 1) * LANES] = piece.astype(BF16)
+
+    load_left.wait()
+    for l in range(legs):
+        for m in range(legs):
+            gap = (link_sm[0, l] - link_sm[0, m]).astype(F32)
+            value = jnp.where(gaps_here == gap, left_v[l * legs + m].astype(F32), 0.0)
+            left_s[pl.ds(l * legs + m, half, stride=pad), 0:chi] = value
+    left_b[...] = left_s[...].astype(BF16)
+
+    def half_one(source):
+        at = pl.multiple_of(source * half, 16)
+        for u in range(legs):
+            for v in range(legs):
+                spread(mps_all[source, u * legs + v].astype(F32), rhs1, at, v * legs + u)
+
+    load_mps.wait()
+    half_one(me_sec)
+
+    pl.semaphore_wait(barrier, secs + 1)
+    charge_copy().start()
+    for k in range(1, secs):
+        mps_copy(k, me_sec).start()
+    for c in range(chunks):
+        right_copy(c).start()
+    tell(0)
 
     small = (pad, 2 * LANES)
     row_in = axis(small, 0)
@@ -145,53 +209,19 @@
     tall_top = over(tall_col, pad)
     tall_mid = over(tall_col - pad * tall_top, legs)
     spread_c = jnp.where(jnp.logical_and(tall_u == tall_top, tall_l == tall_mid), 1.0, 0.0).astype(BF16)
-    ket = ket_ref[...]
-    for r in range(legs):
-        lead = jnp.where(axis((pad, legs), 1) == float(r), 1.0, 0.0).astype(BF16)
-        grown = lax.dot_general(lead, ket, (((1,), (1,)), ((), ())), preferred_element_type=F32)
-        for p in range(phys):
-            keep = jnp.logical_and(line_d == row_last[:, 0:1], line_p == float(p))
-            picked = jnp.where(keep, grown, 0.0).astype(BF16)
-            raw_s[p, r * pad : (r + 1) * pad, :] = jnp.dot(picked, spread_c, preferred_element_type=F32)
-
-    load_left.wait()
-    for l in range(legs):
-        for m in range(legs):
-            gap = (link_sm[0, l] - link_sm[0, m]).astype(F32)
-            value = jnp.where(gaps_here == gap, left_v[l * legs + m].astype(F32), 0.0)
-            left_s[pl.ds(l * legs + m, half, stride=pad), 0:chi] = value
-    left_b[...] = left_s[...].astype(BF16)
-
-    pl.semaphore_wait(barrier, total - 1)
-    charge_copy().start()
+    lead = jnp.where(over(axis((deep, legs), 0), pad) == axis((deep, legs), 1), 1.0, 0.0).astype(BF16)
+    grown = lax.dot_general(lead, ket_ref[...], (((1,), (1,)), ((), ())), preferred_element_type=F32)
+    same_d = line_d == row_last[:, 0:1]
+    for p in range(phys):
+        keep = jnp.logical_and(same_d, line_p == float(p))
+        picked = [jnp.where(keep, grown[r * pad : (r + 1) * pad], 0.0) for r in range(legs)]
+        picked = jnp.concatenate(picked, axis=0).astype(BF16)
+        raw_s[p] = jnp.dot(picked, spread_c, preferred_element_type=F32)
+
     for k in range(1, secs):
-        mps_copy(k, me_sec).start()
-    right_copy().start()
-
-    lane = lax.broadcasted_iota(jnp.int32, (1, LANES), 1)
-
-    def inside(lo, hi):
-        return jnp.logical_and(lane >= lo, lane < hi)
-
-    def turned(value):
-        rest = jnp.zeros(value.shape[:-1] + (LANES - chi,), value.dtype)
-        wide = jnp.concatenate([value, rest], axis=1)
-        return [wide if (chi * g) % LANES == 0 else pltpu.roll(wide, (chi * g) % LANES, 1) for g in range(group)]
-
-    def spread(value, dest, at, column):
-        rolled = turned(value)
-        for t in range(tiles):
-            for k, (g, lo, hi) in enumerate(pieces[t]):
-                piece = jnp.where(inside(lo, hi), rolled[g], 0.0)
-                dest[t, k * LANES + at : k * LANES + at + half, column * LANES : (column + 1) * LANES] = piece.astype(BF16)
-
-    load_mps.wait()
-    for k in range(1, secs):
-        mps_copy(k, lax.rem(me_sec + k, secs)).wait_recv()
-    for k in range(secs):
-        for u in range(legs):
-            for v in range(legs):
-                spread(mps_all[k, u * legs + v].astype(F32), rhs1, k * half, v * legs + u)
+        source = lax.rem(me_sec + k, secs)
+        mps_copy(k, source).wait_recv()
+        half_one(source)
 
     for t in range(tiles):
         lhs = jnp.concatenate([left_b[g * block : (g + 1) * block] for g, _, _ in pieces[t]], axis=1)
@@ -207,6 +237,8 @@
 
         lax.fori_loop(0, pairs * legs, first, 0, unroll=True)
 
+    hear(0)
+    tell(1)
     charge_copy().wait_recv()
     after = charge_next[...].astype(F32)
 
@@ -235,8 +267,8 @@
         for q in range(quads):
             key = jnp.zeros((16, LANES), F32)
             for g, lo, hi in pieces[t]:
-                own = diff[pl.ds(me_sec * half + g * quads + q, 1), :]
-                key += jnp.where(inside(lo, hi), turned_next[g] - own, 0.0)
+                fresh = diff[pl.ds(me_sec * half + g * quads + q, 1), :]
+                key += jnp.where(inside(lo, hi), turned_next[g] - fresh, 0.0)
             lanekey[t, q // 2, :, (q % 2) * LANES : (q % 2 + 1) * LANES] = key.astype(BF16)
 
     def second(n, slot):
@@ -271,34 +303,55 @@
         third(n - 1, (n + 1) % 2)
         return 0
 
+    next_rows = down_rows(after[1:2])
+
+    def build(c):
+        for k in range(secs):
+            delta = next_rows[k * half : (k + 1) * half, 0:chi] - after[0:1, 0:chi]
+            for i in range(own):
+                r, s = divmod(c * own + i, legs)
+                gap = after[2:3, r : r + 1] - after[2:3, s : s + 1]
+                value = jnp.where(delta == gap, right_all[k, c, i].astype(F32), 0.0)
+                spread(value, rhs4[c], k * half, i)
+
+    def last(c):
+        seen = set()
+        for t in range(tiles):
+            part = lax.dot_general(
+                w3[t, :, c * own * LANES : (c + 1) * own * LANES], rhs4[c][t],
+                (((1,), (1,)), ((), ())), preferred_element_type=F32,
+            )
+            for k, (g, _, _) in enumerate(pieces[t]):
+                value = part[:, k * LANES : (k + 1) * LANES]
+                if c > 0 or g in seen:
+                    value += image_s[g * block : (g + 1) * block]
+                seen.add(g)
+                image_s[g * block : (g + 1) * block] = value
+
+    stops = [1] + [steps * p // 18 for p in (8, 12, 15)] + [steps]
     second(0, 0)
-    lax.fori_loop(1, steps // 2, middle, 0, unroll=True)
-    right_copy().wait_recv()
-    for k in range(1, secs):
-        right_pass(k, me_sec).start()
-    lax.fori_loop(steps // 2, steps, middle, 0, unroll=True)
+    lax.fori_loop(stops[0], stops[1], middle, 0, unroll=True)
+    hear(1)
+    tell(2)
+    arrived(0)
+    lax.fori_loop(stops[1], stops[2], middle, 0, unroll=True)
+    hear(2)
+    for n in range(3, rounds):
+        tell(n)
+        hear(n)
+    passed(0)
+    build(0)
+    lax.fori_loop(stops[2], stops[3], middle, 0, unroll=True)
+    arrived(1)
+    lax.fori_loop(stops[3], stops[4], middle, 0, unroll=True)
     third(steps - 1, (steps - 1) % 2)
-
-    diff[...] = down_rows(after[1:2]) - after[0:1]
-    for k in range(1, secs):
-        right_pass(k, lax.rem(me_sec + k, secs)).wait_recv()
-    for k in range(secs):
-        delta = diff[k * half : (k + 1) * half, 0:chi]
-        for r in range(legs):
-            for s in range(legs):
-                gap = after[2:3, r : r + 1] - after[2:3, s : s + 1]
-                value = jnp.where(delta == gap, right_all[k, r * legs + s].astype(F32), 0.0)
-                spread(value, rhs4, k * half, r * legs + s)
-
-    seen = set()
-    for t in range(tiles):
-        part = lax.dot_general(w3[t], rhs4[t], (((1,), (1,)), ((), ())), preferred_element_type=F32)
-        for k, (g, _, _) in enumerate(pieces[t]):
-            value = part[:, k * LANES : (k + 1) * LANES]
-            if g in seen:
-                value += image_s[g * block : (g + 1) * block]
-            seen.add(g)
-            image_s[g * block : (g + 1) * block] = value
+    for c in range(1, chunks):
+        passed(c)
+        if c + 1 < chunks:
+            arrived(c + 1)
+        last(c - 1)
+        build(c)
+    last(chunks - 1)
 
     diff[...] = fresh_rows + after[1:2]
     odd = diff[mine, 0:chi]
@@ -313,60 +366,54 @@
             total_sq += value * value
     part = jnp.sum(jnp.sum(total_sq, axis=0, keepdims=True), axis=1, keepdims=True)
     stage[...] = jnp.broadcast_to(part, stage.shape)
-    slots[me] = jnp.broadcast_to(part, stage.shape)
-
-    def copy_to(k):
-        at, where = other(k)
-        return pltpu.make_async_remote_copy(
-            src_ref=stage, dst_ref=slots.at[me], send_sem=send_sem.at[k], recv_sem=recv_sem.at[me],
-            device_id=where, device_id_type=MESH,
+
+    def close_copy(k, source):
+        return pltpu.make_async_remote_copy(
+            src_ref=stage, dst_ref=close_slots.at[source], send_sem=close_send.at[k], recv_sem=close_recv.at[source],
+            device_id=partner(k), device_id_type=MESH,
+        )
+
+    def far_copy(k, d):
+        return pltpu.make_async_remote_copy(
+            src_ref=stage, dst_ref=slots.at[cols - 1 - k, me_sec], send_sem=far_send, recv_sem=far_recv,
+            device_id=(column(k), d), device_id_type=MESH,
+        )
+
+    def far_all():
+        return pltpu.make_async_remote_copy(
+            src_ref=slots, dst_ref=slots, send_sem=far_send, recv_sem=far_recv,
+            device_id=(before, me_sec), device_id_type=MESH,
         )
 
     def send(k, _):
-        copy_to(k).start()
+        for d in range(secs):
+            far_copy(k, d).start()
         return 0
 
-    def receive(k, _):
-        at, where = other(k)
-        pltpu.make_async_remote_copy(
-            src_ref=stage, dst_ref=slots.at[at], send_sem=send_sem.at[k], recv_sem=recv_sem.at[at],
-            device_id=where, device_id_type=MESH,
-        ).wait_recv()
-        return 0
-
-    def sent(k, _):
-        copy_to(k).wait_send()
-        return 0
-
-    lax.fori_loop(1, total, send, 0)
+    for k in range(1, secs):
+        close_copy(k, me_sec).start()
+    lax.fori_loop(1, cols, send, 0, unroll=cols <= 16)
     site = jnp.broadcast_to(part, stage.shape)
     for k in range(1, secs):
-        receive(close(k), 0)
-        site = site + slots[me_col * secs + lax.rem(me_sec + k, secs)]
+        source = lax.rem(me_sec + k, secs)
+        close_copy(k, source).wait_recv()
+        site = site + close_slots[source]
     scale = lax.rsqrt(site[0:1, 0:1] / count + 1e-06)
     for i in range(square):
         out_ref[i] = (clean_s[i] * scale).astype(BF16)
-
-    def receive_far(k, _):
-        at, _where = other(k)
-
-        @pl.when(at // secs != me_col)
-        def _():
-            receive(k, 0)
-
-        return 0
-
-    lax.fori_loop(1, total, receive_far, 0)
-    sums = jnp.sum(slots[...].reshape(cols, secs, 1, LANES), axis=1) / count
-    logs = jnp.sum(0.5 * jnp.log(sums + 1e-06), axis=0) / cols
-    log_ref[...] = logs[0:1, 0:1]
-    lax.fori_loop(1, total, sent, 0)
     charge_copy().wait_send()
     for k in range(1, secs):
         mps_copy(k, me_sec).wait_send()
-    right_copy().wait_send()
-    for k in range(1, secs):
-        right_pass(k, me_sec).wait_send()
+        close_copy(k, me_sec).wait_send()
+        for c in range(chunks):
+            right_pass(c, k, me_sec).wait_send()
+    for c in range(chunks):
+        right_copy(c).wait_send()
+    far_all().wait_recv()
+    sums = jnp.sum(slots[...], axis=1) / count
+    logs = jnp.sum(0.5 * jnp.log(sums + 1e-06), axis=0) + 0.5 * jnp.log(site / count + 1e-06)
+    log_ref[...] = logs[0:1, 0:1] / cols
+    far_all().wait_send()
 
 
 def local(mps, ket, left_proj, right_proj, bond_charge, new_charge, link_charge, vert_charge):
@@ -377,6 +424,8 @@
     cols, secs = lax.axis_size("col"), lax.axis_size("sec")
     group, tiles, quads, pad, pieces = layout(chi, half, legs)
     deep, block = legs * pad, quads * pad
+    chunks = 3
+    own = square // chunks
     assert deep <= 2 * LANES
     arrays = [
         left_proj[0].transpose(2, 3, 0, 1).reshape(square, half, chi),
@@ -400,11 +449,11 @@
         scratch_shapes=[
             pltpu.VMEM((square, half, chi), BF16),
             pltpu.VMEM((secs, square, half, chi), BF16),
-            pltpu.VMEM((secs, square, half, chi), BF16),
+            pltpu.VMEM((secs, chunks, own, half, chi), BF16),
             pltpu.VMEM((half * pad, LANES), F32),
             pltpu.VMEM((half * pad, LANES), BF16),
             pltpu.VMEM((tiles, 2 * LANES, square * LANES), BF16),
-            pltpu.VMEM((tiles, 2 * LANES, square * LANES), BF16),
+            [pltpu.VMEM((tiles, 2 * LANES, own * LANES), BF16) for _ in range(chunks)],
             pltpu.VMEM((phys, deep, 2 * LANES), F32),
             pltpu.VMEM((deep, 2 * LANES), F32),
             pltpu.VMEM((tiles, quads // 2, legs, deep, 2 * LANES), BF16),
@@ -418,12 +467,20 @@
             pltpu.VMEM((legs, deep, LANES), BF16),
             pltpu.VMEM((tiles, quads // 2, 16, 2 * LANES), BF16),
             pltpu.VMEM((1, LANES), F32),
-            pltpu.VMEM((cols * secs, 1, LANES), F32),
+            pltpu.VMEM((cols - 1, secs, 1, LANES), F32),
+            pltpu.VMEM((secs, 1, LANES), F32),
             pltpu.SemaphoreType.DMA((2,)),
-            pltpu.SemaphoreType.DMA((2 * secs,)),
-            pltpu.SemaphoreType.DMA((1 + 2 * secs,)),
-            pltpu.SemaphoreType.DMA((cols * secs,)),
-            pltpu.SemaphoreType.DMA((cols * secs,)),
+            pltpu.SemaphoreType.DMA((secs,)),
+            pltpu.SemaphoreType.DMA((1 + secs,)),
+            pltpu.SemaphoreType.DMA((chunks,)),
+            pltpu.SemaphoreType.DMA((chunks,)),
+            pltpu.SemaphoreType.DMA((chunks, secs)),
+            pltpu.SemaphoreType.DMA((chunks, secs)),
+            pltpu.SemaphoreType.REGULAR((max(1, (cols // 2 - 1).bit_length()),)),
+            pltpu.SemaphoreType.DMA,
+            pltpu.SemaphoreType.DMA,
+            pltpu.SemaphoreType.DMA((secs,)),
+            pltpu.SemaphoreType.DMA((secs,)),
         ],
         compiler_params=pltpu.CompilerParams(
             vmem_limit_bytes=62 * 1024 * 1024,

time: 41.7 us -> 35.6 us (0.85)
  Pallas kernels: 37.3 us -> 31.1 us
    pallas_call x1, Pallas kernels: 37.3 us -> 31.1 us  [local(): pl.pallas_call(functools.partial(chain, legs, phys, chi * square * chi, c...]
where the time goes in v2:
time: 35.6 us; the launch traced here: 35.4 us
  Pallas kernels  31.1 us (87%)
  between operations  2.44 us (7%)
  local copies, waits for them, and re-layouts  1.8 us (5%)
    pallas_call x1, Pallas kernels, local(): pl.pallas_call(functools.partial(chain, legs, phys, chi * square * chi, c...  31.1 us
    unnamed x1, local copies, waits for them, and re-layouts  1.8 us

profile of v2, /device:TPU:0, one launch (start us, length us, event | category | flops | bytes accessed | tf_op | source)
XLA Modules:
  0.0 35.4 jit_solution(13323841752521839441)
XLA Ops:
  0.6 31.1 %shard_map.95 = (bf16[36,48,96]{2,1,0:T(8,128)(2,1)}, f32[1,1]{1,0:T(1,128)}) custom-call(bf16[36,48,96]{2,1,0:T(8,128)(2,1)} %bitcast.27, bf16[36,48,96]{2,1,0:T(8,128)(2,1)} %bitcast.28, bf16[36,48,96]{2,1,0:T(8,128)(2,1)} %bitcast.29, bf16[432,6]{1,0:T(8,128)(2,1)} %bitcast.31, s32[1,96]{1,0:T(1,128)} %bond_ref.1, s32[1,96]{1,0:T(1,128)} %fresh_ref.1, ...), custom_call_target="tpu_custom_call" | custom-call | tf_op jit(solution)/shard_map/pallas_call | solution.py:444
  31.8 1.8 %copy.12 = bf16[1,48,6,6,96]{4,1,3,2,0:T(8,128)(2,1)} copy(bf16[1,48,6,6,96]{4,1,3,2,0:T(8,128)(2,1)} %bitcast.30) | data formatting | bytes 663552

commit v3 on v2

--- a/solution.py
+++ b/solution.py
@@ -33,9 +33,9 @@
 
 def chain(
     legs, phys, count, cols, secs,
-    left_hbm, mps_hbm, right_hbm, ket_ref, bond_ref, fresh_ref, link_ref, link_sm, vert_sm,
+    left_hbm, mps_hbm, right_hbm, ket_hbm, bond_hbm, fresh_hbm, link_hbm, link_far, vert_far,
     out_ref, log_ref,
-    left_v, mps_all, right_all, left_s, left_b, rhs1, rhs4, raw_s, whole_s, w1, w2, w3, image_s, clean_s,
+    ket_ref, bond_ref, fresh_ref, link_ref, link_sm, vert_sm, right_v, left_v, mps_all, right_all, left_s, left_b, rhs1, rhs4, raw_s, whole_s, w1, w2, w3, image_s, clean_s,
     charge_here, charge_next, diff, rowkey, lanekey,
     stage, slots, close_slots, local_sem, near_send, near_recv, chunk_send, chunk_recv, pass_send, pass_recv,
     known, far_send, far_recv, close_send, close_recv,
@@ -68,14 +68,14 @@
 
     def mps_copy(k, source):
         return pltpu.make_async_remote_copy(
-            src_ref=mps_hbm, dst_ref=mps_all.at[source], send_sem=near_send.at[k],
+            src_ref=mps_all.at[source], dst_ref=mps_all.at[source], send_sem=near_send.at[k],
             recv_sem=near_recv.at[1 + source],
             device_id=partner(k), device_id_type=MESH,
         )
 
     def right_copy(c):
         return pltpu.make_async_remote_copy(
-            src_ref=right_hbm.at[pl.ds(c * own, own)], dst_ref=right_all.at[me_sec, c],
+            src_ref=right_v.at[pl.ds(c * own, own)], dst_ref=right_all.at[me_sec, c],
             send_sem=chunk_send.at[c], recv_sem=chunk_recv.at[c],
             device_id=(before, me_sec), device_id_type=MESH,
         )
@@ -121,15 +121,24 @@
     def chosen(index, values):
         return sum(jnp.where(index == float(i), v, 0.0) for i, v in enumerate(values))
 
-    load_left = pltpu.make_async_copy(left_hbm, left_v, local_sem.at[0])
-    load_mps = pltpu.make_async_copy(mps_hbm, mps_all.at[me_sec], local_sem.at[1])
-    load_left.start()
-    load_mps.start()
-
     for k in range(1, secs):
         pl.semaphore_signal(barrier, inc=1, device_id=partner(k), device_id_type=MESH)
     for side in (-1, 1):
         pl.semaphore_signal(barrier, inc=1, device_id=(column(side), me_sec), device_id_type=MESH)
+    load_left = pltpu.make_async_copy(left_hbm, left_v, local_sem.at[0])
+    load_mps = pltpu.make_async_copy(mps_hbm, mps_all.at[me_sec], local_sem.at[1])
+    small = [(bond_hbm, bond_ref), (fresh_hbm, fresh_ref), (link_hbm, link_ref), (link_far, link_sm), (vert_far, vert_sm)]
+    small = [pltpu.make_async_copy(a, b, local_sem.at[3 + i]) for i, (a, b) in enumerate(small)]
+    load_right = pltpu.make_async_copy(right_hbm, right_v, local_sem.at[8])
+    load_ket = pltpu.make_async_copy(ket_hbm, ket_ref, local_sem.at[2])
+    for copy in small + [load_left, load_mps, load_ket, load_right]:
+        copy.start()
+    left_s[...] = jnp.zeros_like(left_s)
+    for t in range(tiles):
+        for k in range(2):
+            rhs1[t, k * LANES + chi : (k + 1) * LANES] = jnp.zeros((LANES - chi, square * LANES), BF16)
+    for copy in small:
+        copy.wait()
     charge_here[...] = jnp.zeros_like(charge_here)
     charge_here[0:1, 0:chi] = bond_ref[...]
     charge_here[1:2, 0:chi] = fresh_ref[...]
@@ -138,13 +147,6 @@
     diff[...] = down_rows(here[1:2]) - here[0:1]
     gaps_here = diff[mine, 0:chi]
     fresh_rows = down_rows(here[1:2])
-    left_s[...] = jnp.zeros_like(left_s)
-    for t in range(tiles):
-        for k in range(2):
-            rhs1[t, k * LANES + chi : (k + 1) * LANES] = jnp.zeros((LANES - chi, square * LANES), BF16)
-            for c in range(chunks):
-                rhs4[c][t, k * LANES + chi : (k + 1) * LANES] = jnp.zeros((LANES - chi, own * LANES), BF16)
-
     lane = lax.broadcasted_iota(jnp.int32, (1, LANES), 1)
 
     def inside(lo, hi):
@@ -178,14 +180,6 @@
 
     load_mps.wait()
     half_one(me_sec)
-
-    pl.semaphore_wait(barrier, secs + 1)
-    charge_copy().start()
-    for k in range(1, secs):
-        mps_copy(k, me_sec).start()
-    for c in range(chunks):
-        right_copy(c).start()
-    tell(0)
 
     small = (pad, 2 * LANES)
     row_in = axis(small, 0)
@@ -209,6 +203,7 @@
     tall_top = over(tall_col, pad)
     tall_mid = over(tall_col - pad * tall_top, legs)
     spread_c = jnp.where(jnp.logical_and(tall_u == tall_top, tall_l == tall_mid), 1.0, 0.0).astype(BF16)
+    load_ket.wait()
     lead = jnp.where(over(axis((deep, legs), 0), pad) == axis((deep, legs), 1), 1.0, 0.0).astype(BF16)
     grown = lax.dot_general(lead, ket_ref[...], (((1,), (1,)), ((), ())), preferred_element_type=F32)
     same_d = line_d == row_last[:, 0:1]
@@ -217,6 +212,15 @@
         picked = [jnp.where(keep, grown[r * pad : (r + 1) * pad], 0.0) for r in range(legs)]
         picked = jnp.concatenate(picked, axis=0).astype(BF16)
         raw_s[p] = jnp.dot(picked, spread_c, preferred_element_type=F32)
+
+    load_right.wait()
+    pl.semaphore_wait(barrier, secs + 1)
+    charge_copy().start()
+    for k in range(1, secs):
+        mps_copy(k, me_sec).start()
+    for c in range(chunks):
+        right_copy(c).start()
+    tell(0)
 
     for k in range(1, secs):
         source = lax.rem(me_sec + k, secs)
@@ -305,28 +309,27 @@
 
     next_rows = down_rows(after[1:2])
 
-    def build(c):
-        for k in range(secs):
-            delta = next_rows[k * half : (k + 1) * half, 0:chi] - after[0:1, 0:chi]
-            for i in range(own):
-                r, s = divmod(c * own + i, legs)
-                gap = after[2:3, r : r + 1] - after[2:3, s : s + 1]
-                value = jnp.where(delta == gap, right_all[k, c, i].astype(F32), 0.0)
-                spread(value, rhs4[c], k * half, i)
-
-    def last(c):
-        seen = set()
-        for t in range(tiles):
-            part = lax.dot_general(
-                w3[t, :, c * own * LANES : (c + 1) * own * LANES], rhs4[c][t],
-                (((1,), (1,)), ((), ())), preferred_element_type=F32,
-            )
-            for k, (g, _, _) in enumerate(pieces[t]):
-                value = part[:, k * LANES : (k + 1) * LANES]
-                if c > 0 or g in seen:
-                    value += image_s[g * block : (g + 1) * block]
-                seen.add(g)
-                image_s[g * block : (g + 1) * block] = value
+    def build(c, k, i):
+        delta = next_rows[k * half : (k + 1) * half, 0:chi] - after[0:1, 0:chi]
+        r, s = divmod(c * own + i, legs)
+        gap = after[2:3, r : r + 1] - after[2:3, s : s + 1]
+        value = jnp.where(delta == gap, right_all[k, c, i].astype(F32), 0.0)
+        spread(value, rhs4[c], k * half, i)
+
+    def share(c, n, of):
+        for at in range(secs * own * n // of, secs * own * (n + 1) // of):
+            build(c, at // own, at % own)
+
+    def last(c, t):
+        part = lax.dot_general(
+            w3[t, :, c * own * LANES : (c + 1) * own * LANES], rhs4[c][t],
+            (((1,), (1,)), ((), ())), preferred_element_type=F32,
+        )
+        for k, (g, _, _) in enumerate(pieces[t]):
+            value = part[:, k * LANES : (k + 1) * LANES]
+            if c > 0 or k == 0 and t > 0:
+                value += image_s[g * block : (g + 1) * block]
+            image_s[g * block : (g + 1) * block] = value
 
     stops = [1] + [steps * p // 18 for p in (8, 12, 15)] + [steps]
     second(0, 0)
@@ -340,18 +343,24 @@
         tell(n)
         hear(n)
     passed(0)
-    build(0)
-    lax.fori_loop(stops[2], stops[3], middle, 0, unroll=True)
-    arrived(1)
-    lax.fori_loop(stops[3], stops[4], middle, 0, unroll=True)
+    of = 2 * (steps - stops[2])
+    for n in range(stops[2], steps):
+        if n == stops[3]:
+            arrived(1)
+        second(n, n % 2)
+        share(0, 2 * (n - stops[2]), of)
+        third(n - 1, (n + 1) % 2)
+        share(0, 2 * (n - stops[2]) + 1, of)
     third(steps - 1, (steps - 1) % 2)
     for c in range(1, chunks):
         passed(c)
         if c + 1 < chunks:
             arrived(c + 1)
-        last(c - 1)
-        build(c)
-    last(chunks - 1)
+        for t in range(tiles):
+            share(c, t, tiles)
+            last(c - 1, t)
+    for t in range(tiles):
+        last(chunks - 1, t)
 
     diff[...] = fresh_rows + after[1:2]
     odd = diff[mine, 0:chi]
@@ -440,13 +449,19 @@
     ]
     far = pl.BlockSpec(memory_space=pl.ANY)
     near = pl.BlockSpec(memory_space=pltpu.VMEM)
-    scalar = pl.BlockSpec(memory_space=pltpu.SMEM)
     image, logs = pl.pallas_call(
         functools.partial(chain, legs, phys, chi * square * chi, cols, secs),
-        in_specs=[far] * 3 + [near] * 4 + [scalar] * 2,
+        in_specs=[far] * len(arrays),
         out_specs=[near, near],
-        out_shape=[jax.ShapeDtypeStruct((square, half, chi), BF16), jax.ShapeDtypeStruct((1, 1), F32)],
+        out_shape=[pltpu.VMEM((square, half, chi), BF16), jax.ShapeDtypeStruct((1, 1), F32)],
         scratch_shapes=[
+            pltpu.VMEM(arrays[3].shape, BF16),
+            pltpu.VMEM((1, chi), jnp.int32),
+            pltpu.VMEM((1, chi), jnp.int32),
+            pltpu.VMEM((1, legs), jnp.int32),
+            pltpu.SMEM((1, legs), jnp.int32),
+            pltpu.SMEM((2, legs), jnp.int32),
+            pltpu.VMEM((square, half, chi), BF16),
             pltpu.VMEM((square, half, chi), BF16),
             pltpu.VMEM((secs, square, half, chi), BF16),
             pltpu.VMEM((secs, chunks, own, half, chi), BF16),
@@ -469,7 +484,7 @@
             pltpu.VMEM((1, LANES), F32),
             pltpu.VMEM((cols - 1, secs, 1, LANES), F32),
             pltpu.VMEM((secs, 1, LANES), F32),
-            pltpu.SemaphoreType.DMA((2,)),
+            pltpu.SemaphoreType.DMA((9,)),
             pltpu.SemaphoreType.DMA((secs,)),
             pltpu.SemaphoreType.DMA((1 + secs,)),
             pltpu.SemaphoreType.DMA((chunks,)),
@@ -483,7 +498,7 @@
             pltpu.SemaphoreType.DMA((secs,)),
         ],
         compiler_params=pltpu.CompilerParams(
-            vmem_limit_bytes=62 * 1024 * 1024,
+            vmem_limit_bytes=60 * 1024 * 1024,
             collective_id=0,
             has_side_effects=True,
         ),

time: 35.6 us -> 33.5 us (0.941)
  local copies, waits for them, and re-layouts: 1.8 us -> 0.76 us
  Pallas kernels: 31.1 us -> 30.3 us
    unnamed x1, local copies, waits for them, and re-layouts: 1.8 us -> 0.76 us
    pallas_call x1, Pallas kernels: 31.1 us -> 30.3 us  [local(): pl.pallas_call(functools.partial(chain, legs, phys, chi * square * chi, c...]
where the time goes in v3:
time: 33.5 us; the launch traced here: 33.4 us
  Pallas kernels  30.3 us (90%)
  between operations  2.33 us (7%)
  local copies, waits for them, and re-layouts  0.76 us (2%)
    pallas_call x1, Pallas kernels, local(): pl.pallas_call(functools.partial(chain, legs, phys, chi * square * chi, c...  30.3 us
    unnamed x1, local copies, waits for them, and re-layouts  0.76 us

profile of v3, /device:TPU:0, one launch (start us, length us, event | category | flops | bytes accessed | tf_op | source)
XLA Modules:
  0.0 33.4 jit_solution(6428116366163970590)
XLA Ops:
  0.6 30.3 %shard_map.95 = (bf16[36,48,96]{2,1,0:T(8,128)(2,1)S(1)}, f32[1,1]{1,0:T(1,128)}) custom-call(bf16[36,48,96]{2,1,0:T(8,128)(2,1)} %bitcast.28, bf16[36,48,96]{2,1,0:T(8,128)(2,1)} %bitcast.29, bf16[36,48,96]{2,1,0:T(8,128)(2,1)} %bitcast.30, bf16[432,6]{1,0:T(8,128)(2,1)} %bitcast.31, s32[1,96]{1,0:T(1,128)} %bond_hbm.1, s32[1,96]{1,0:T(1,128)} %fresh_hbm.1, ...), custom_call_target="tpu_custom_call" | custom-call | tf_op jit(solution)/shard_map/pallas_call | solution.py:452
  30.9 0.8 %copy.12 = bf16[1,48,6,6,96]{4,1,3,2,0:T(8,128)(2,1)} copy(bf16[1,48,6,6,96]{4,1,3,2,0:T(8,128)(2,1)S(1)} %bitcast.27) | data formatting | bytes 663552
